TPU v7x, 32 devices: a whole 2x2x4 slice. The times are simulated.
32 devices in a mesh: tok: 8 (over z, y), head: 4 (over x, core).
Axes of the slice: x: 2, y: 2, z: 4, core: 2. Of those that a mesh axis runs over, the one named last changes fastest.
Arguments:
- query_rows: bfloat16 [4096, 4, 1024], P('tok', 'head'), may hold values from -6 to 6
- key_rows: bfloat16 [4096, 4, 128], P('tok', 'head'), may hold values from -6 to 6
- value_rows: bfloat16 [4096, 4, 128], P('tok', 'head'), may hold values from -6 to 6
- output_gradient: bfloat16 [4096, 4, 1024], P('tok', 'head'), may hold values from -6 to 6
- row_logsumexp: bfloat16 [4, 8, 4096], P('head', None, 'tok'), may hold values from 3 to 7
- row_delta_sums: bfloat16 [4, 8, 4096], P('head', None, 'tok'), may hold values from -5 to 5
- segments: int32 [4096], replicated, may hold values from 0 to 4095, as said below
- query_key_value_weight: bfloat16 [4096, 4, 1280], P('tok', 'head'), may hold values from -0.09375 to 0.09375
Outputs:
- grad_input: bfloat16 [4096, 4096], P('tok', 'head')
Inputs may be any that keep to these rules, and one draw needn't show every extreme that they name: `segments`: numbers never fall along the tokens, and every document lies inside one window of 512 consecutive tokens.
All inputs are finite; a program needn't handle non-finite values.
Results may differ from a plain program's by a relative error of at most 0.012.
Values may be sent and summed in bfloat16 or wider, within the bound.
A program may use at most 128 MiB of HBM per device.

v0:
```python
import jax
import jax.numpy as jnp
import numpy as np
from jax import lax
from jax.sharding import PartitionSpec as P

BLOCK = 128


def pair_lists(block_count):
    query_list = []
    key_list = []
    for query_block in range(block_count):
        for key_block in range(query_block + 1):
            query_list.append(query_block)
            key_list.append(key_block)
    return (np.array(query_list, np.int32), np.array(key_list, np.int32))


def live_pairs(seg_window, query_list, key_list, tile_rows):
    first_seg = jnp.take(seg_window, query_list * tile_rows)
    last_seg = jnp.take(seg_window, key_list * tile_rows + tile_rows - 1)
    return (first_seg == last_seg) | jnp.asarray(query_list == key_list)


def pair_grads(query_tile, dout_tile, key_tile, value_tile, lse_tile, delta_tile, allowed):
    tile_rows, groups, query_width = query_tile.shape
    head_size = key_tile.shape[2]
    heads_per_group = query_width // head_size
    query_heads = query_tile.reshape(tile_rows, groups, heads_per_group, head_size)
    dout_heads = dout_tile.reshape(tile_rows, groups, heads_per_group, head_size)
    scores = jnp.einsum(
        "agrd,bgd->grab", query_heads, key_tile, preferred_element_type=jnp.float32
    ) * head_size ** (-0.5)
    logits = scores - lse_tile.astype(jnp.float32)[:, :, :, None]
    soft_probs = jnp.where(allowed[None, None], jnp.exp(logits), 0.0)
    probs_low = soft_probs.astype(jnp.bfloat16)
    value_gradient = jnp.einsum(
        "grab,agrd->bgd", probs_low, dout_heads, preferred_element_type=jnp.float32
    )
    grad_prob = jnp.einsum(
        "agrd,bgd->grab", dout_heads, value_tile, preferred_element_type=jnp.float32
    )
    grad_score = (soft_probs * (grad_prob - delta_tile.astype(jnp.float32)[:, :, :, None])).astype(
        jnp.bfloat16
    )
    query_gradient = jnp.einsum(
        "grab,bgd->agrd", grad_score, key_tile, preferred_element_type=jnp.float32
    )
    key_gradient = jnp.einsum(
        "grab,agrd->bgd", grad_score, query_heads, preferred_element_type=jnp.float32
    )
    return (query_gradient.reshape(tile_rows, groups, query_width), key_gradient, value_gradient)


def on_device(
    query_rows,
    key_rows,
    value_rows,
    output_gradient,
    row_logsumexp,
    row_delta_sums,
    segments,
    query_key_value_weight,
):
    window, kv_dev, query_width = query_rows.shape
    head_size = key_rows.shape[2]
    tile_rows = BLOCK
    block_count = window // tile_rows
    query_list, key_list = pair_lists(block_count)
    query_table = jnp.asarray(query_list)
    key_table = jnp.asarray(key_list)
    myself = lax.axis_index("tok")
    own_seg = lax.dynamic_slice_in_dim(segments, myself * window, window)
    own_live = live_pairs(own_seg, query_list, key_list, tile_rows)
    block_ids = jnp.arange(block_count, dtype=jnp.int32)
    query_match = (query_table[:, None] == block_ids[None, :]) & own_live[:, None]
    key_match = key_table[:, None] == block_ids[None, :]
    block_local = jnp.any(query_match[:, :, None] & key_match[:, None, :], axis=0)
    token_local = jnp.repeat(jnp.repeat(block_local, tile_rows, axis=0), tile_rows, axis=1)
    offsets = jnp.arange(window, dtype=jnp.int32)
    allowed_all = (
        (own_seg[:, None] == own_seg[None, :])
        & (offsets[None, :] <= offsets[:, None])
        & token_local
    )
    local_out = pair_grads(
        query_rows,
        output_gradient,
        key_rows,
        value_rows,
        row_logsumexp,
        row_delta_sums,
        allowed_all,
    )
    acc_query = local_out[0].reshape(block_count, tile_rows, kv_dev, query_width)
    acc_key = local_out[1].reshape(block_count, tile_rows, kv_dev, head_size)
    acc_value = local_out[2].reshape(block_count, tile_rows, kv_dev, head_size)
    score_scale = head_size ** (-0.5)
    query_gradient = (acc_query * score_scale).reshape(window, kv_dev, query_width)
    key_gradient = (acc_key * score_scale).reshape(window, kv_dev, head_size)
    value_gradient = acc_value.reshape(window, kv_dev, head_size)
    stacked_gradients = (
        jnp.concatenate([query_gradient, key_gradient, value_gradient], axis=2)
        .astype(jnp.bfloat16)
        .reshape(window, -1)
    )
    weight_piece = lax.all_gather(query_key_value_weight, "tok", axis=0, tiled=True)
    flat_piece = weight_piece.reshape(weight_piece.shape[0], -1)
    partial_sum = lax.dot_general(
        stacked_gradients, flat_piece, (((1,), (1,)), ((), ())), preferred_element_type=jnp.float32
    )
    summed = lax.psum_scatter(
        partial_sum.astype(jnp.bfloat16), "head", scatter_dimension=1, tiled=True
    )
    return summed


def solution(mesh):
    placed = (
        P("tok", "head", None),
        P("tok", "head", None),
        P("tok", "head", None),
        P("tok", "head", None),
        P("head", None, "tok"),
        P("head", None, "tok"),
        P(),
        P("tok", "head", None),
    )
    return jax.shard_map(
        on_device, mesh=mesh, in_specs=placed, out_specs=P("tok", "head"), check_vma=False
    )
```

profile of v0, /device:TPU:24, one launch (start us, length us, event | category | flops | bytes accessed | tf_op | source)
XLA Modules:
  0.0 221.9 jit_solution(3614440104101419879)
XLA Ops:
  6.5 0.0 copy-start
  6.5 0.0 copy-start.1
  6.5 0.0 all-gather.2.cloned.1.call-start
  6.5 0.7 all-gather.2.cloned.1.call-update
  7.3 0.0 reduce-scatter.2.cloned.1.call-start
  7.3 0.8 dynamic_slice.3
  8.1 0.7 pad_clamp_fusion.1
  8.7 0.7 gather_fusion
  9.4 0.7 pad_clamp_fusion
  10.1 0.7 gather_fusion.1
  10.7 0.7 compare_or_fusion
  11.4 0.7 iota_compare_fusion.1
  12.1 0.2 and_reduce_fusion
  12.2 0.1 copy.22
  12.3 0.1 broadcast_bitcast_fusion
  12.4 0.2 fusion.29
  12.7 1.5 copy.36
  14.2 1.5 copy.37
  15.7 0.7 bitcast_convert_fusion.1
  16.4 0.7 bitcast_convert_fusion
  17.1 0.0 copy-done
  17.1 1.2 fusion.32
  18.3 0.0 copy-done.1
  18.3 2.8 %fusion.11 = bf16[8,512,512]{1,2,0:T(8,128)(2,1)S(1)} fusion(f32[512,512,8]{1,0,2:T(8,128)S(1)} %fusion.32, f32[8,512]{1,0:T(8,128)S(1)} %bitcast_convert_fusion, f32[8,512]{1,0:T(8,128)S(1)} %bitcast_convert_fusion.1, pred[512,512]{0,1:T(8,128)(4,1)S(1)} %fusion.29, bf16[512,8,128]{0,2,1:T(8,128)(2,1)S(1)} %bitcast.99, bf16[512,1,128]{2,0,1:T(8,128)(2,1)S(1)} %copy-done.1), kind=kOutput, calls=%fused_computation.13 | convolution fusion | flops 549453824 | bytes 14057472 | tf_op jit(solution)/shard_map/agrd,bgd->grab/dot_general | solution.py:41
  21.2 0.8 multiply_convert_fusion
  22.0 2.1 fusion.27
  24.1 0.0 copy-start.2
  24.1 1.9 fusion.24
  26.1 133.1 %all-gather.2.cloned.1.call-done = bf16[4096,1,1280]{2,0,1:T(8,128)(2,1)} async-done(((bf16[512,1,1280]{2,0,1:T(8,128)(2,1)}), bf16[4096,1,1280]{2,0,1:T(8,128)(2,1)}) %all-gather.2.cloned.1.call-update) | async-done | bytes 10485776 | tf_op jit(solution)/shard_map/all_gather | solution.py:108
  159.1 0.0 copy-done.2
  159.1 11.2 %fusion.7 = bf16[512,4096]{1,0:T(8,128)(2,1)} fusion(bf16[4096,1,1280]{2,0,1:T(8,128)(2,1)} %all-gather.2.cloned.1.call-done, bf16[512,128]{0,1:T(8,128)(2,1)S(1)} %fusion.24, bf16[512,128]{0,1:T(8,128)(2,1)S(1)} %copy-done.2, bf16[512,1024]{0,1:T(8,128)(2,1)S(1)} %bitcast.101), kind=kOutput, calls=%fused_computation.11 | convolution fusion | flops 5374738432 | bytes 15990784 | tf_op jit(solution)/shard_map/dot_general | solution.py:110
  170.3 0.0 reduce-scatter.2.cloned.1.call-update
  170.4 44.7 %reduce-scatter.2.cloned.1.call-done = bf16[512,1024]{1,0:T(8,128)(2,1)} async-done(((bf16[512,4096]{1,0:T(8,128)(2,1)}), bf16[512,1024]{1,0:T(8,128)(2,1)}) %reduce-scatter.2.cloned.1.call-update) | async-done | bytes 1048592 | tf_op jit(solution)/shard_map/reduce_scatter | solution.py:113
  (1 shorter events, 0.0 us)
Async XLA Ops:
  6.5 10.5 %copy-start = (bf16[512,1,128]{2,0,1:T(8,128)(2,1)S(1)}, bf16[512,1,128]{2,0,1:T(8,128)(2,1)}, u32[]{:S(2)}) copy-start(bf16[512,1,128]{2,0,1:T(8,128)(2,1)} %param.16) | copy-start | bytes 393220
  6.5 11.8 %copy-start.1 = (bf16[512,1,128]{2,0,1:T(8,128)(2,1)S(1)}, bf16[512,1,128]{2,0,1:T(8,128)(2,1)}, u32[]{:S(2)}) copy-start(bf16[512,1,128]{2,0,1:T(8,128)(2,1)} %param.17) | copy-start | bytes 393220
  6.5 152.6 %all-gather.2.cloned.1.call-start = ((), (), s32[]{:S(2)}) async-start(), calls=%async_computation.1 | async-start | bytes 11796480 | tf_op jit(solution)/shard_map/all_gather | solution.py:108
  7.3 207.8 %reduce-scatter.2.cloned.1.call-start = ((), (), s32[]{:S(2)}) async-start(), calls=%async_computation.2 | async-start | bytes 5242880 | tf_op jit(solution)/shard_map/reduce_scatter | solution.py:113
  24.1 135.0 %copy-start.2 = (bf16[512,128]{0,1:T(8,128)(2,1)S(1)}, bf16[512,128]{0,1:T(8,128)(2,1)}, u32[]{:S(2)}) copy-start(bf16[512,128]{0,1:T(8,128)(2,1)} %fusion.27) | copy-start | bytes 393220
Sparse Core Ops, SparseCore 0:
  9.5 149.5 all-gather.1
  170.5 44.5 reduce-scatter.1
where the time goes:
time: 224 us; the launch traced here: 222 us
  waiting for transfers between devices  178 us (79%)
  matrix products  20.2 us (9%)
  between operations  13.5 us (6%)
  local copies, waits for them, and re-layouts  5.3 us (2%)
  other arithmetic  4.45 us (2%)
    all_gather x1, waiting for transfers between devices, on_device(): lax.all_gather(query_key_value_weight, 'tok', axis=0, tiled=True)  133 us
    reduce_scatter x1, waiting for transfers between devices, on_device(): lax.psum_scatter(partial_sum.astype(jnp.bfloat16), 'head', scatter_dimens...  44.7 us
    dot_general x1, matrix products, on_device(): lax.dot_general(stacked_gradients, flat_piece, (((1,), (1,)), ((), ())),...  11.2 us
  transfers between devices with their start and end apart: 2, of which 2 were waited for; matrix products, arithmetic and copies ran while one was open for 8% of the time, Pallas kernels for 0%

commit v1 on v0

--- a/solution.py
+++ b/solution.py
@@ -1,7 +1,11 @@
+import functools
+
 import jax
 import jax.numpy as jnp
 import numpy as np
 from jax import lax
+from jax.experimental import pallas as pl
+from jax.experimental.pallas import tpu as pltpu
 from jax.sharding import PartitionSpec as P
 
 BLOCK = 128
@@ -116,6 +120,318 @@
     return summed
 
 
+MESH = pl.DeviceIdType.MESH
+LANES = 128
+
+
+def fused_kernel(
+    inner,
+    q_ref,
+    k_ref,
+    v_ref,
+    do_ref,
+    lse_ref,
+    delta_ref,
+    seg_ref,
+    w_ref,
+    out_ref,
+    joined,
+    w_all,
+    part,
+    got,
+    fwd_out,
+    fwd_in,
+    bias,
+    lse32,
+    delta32,
+    dk_acc,
+    dv_acc,
+    w_send,
+    w_recv,
+    j_send,
+    j_recv,
+    p_send,
+    p_recv,
+    f_send,
+    f_recv,
+):
+    outer, chunks = w_all.shape[0], w_all.shape[1]
+    heads = outer
+    window, head_size = k_ref.shape
+    groups = q_ref.shape[1] // head_size
+    rows = w_ref.shape[0]
+    tok, h = lax.axis_index("tok"), lax.axis_index("head")
+    z, y = tok // inner, tok % inner
+    yo = inner - 1 - y
+
+    def remote(src, dst, send, recv, to_tok, to_head):
+        return pltpu.make_async_remote_copy(
+            src_ref=src,
+            dst_ref=dst,
+            send_sem=send,
+            recv_sem=recv,
+            device_id=(to_tok, to_head),
+            device_id_type=MESH,
+        )
+
+    def peer(step):
+        return lax.rem(h + step, heads)
+
+    barrier = pltpu.get_barrier_semaphore()
+    pl.semaphore_signal(barrier, inc=1, device_id=(z * inner + yo, h), device_id_type=MESH)
+    for step in range(1, heads):
+        pl.semaphore_signal(barrier, inc=1, device_id=(tok, peer(step)), device_id_type=MESH)
+
+    @pl.when(z > 0)
+    def _():
+        pl.semaphore_signal(barrier, inc=1, device_id=(tok - inner, h), device_id_type=MESH)
+
+    @pl.when(z < outer - 1)
+    def _():
+        pl.semaphore_signal(barrier, inc=1, device_id=(tok + inner, h), device_id_type=MESH)
+
+    edges = jnp.where(z > 0, 1, 0) + jnp.where(z < outer - 1, 1, 0)
+    pl.semaphore_wait(barrier, heads + edges)
+
+    def own_w(c):
+        return pl.ds(pl.multiple_of(c * LANES, LANES), LANES)
+
+    def w_copy(side, o, c, own):
+        src = w_ref.at[own_w(c)] if own else w_all.at[o, c]
+        move = 1 if side == 1 else -1
+        return remote(
+            src, w_all.at[o, c], w_send.at[side, o, c], w_recv.at[o, c], tok + move * inner, h
+        )
+
+    def can_send(side):
+        return z < outer - 1 if side == 1 else z > 0
+
+    def each_chunk(body):
+        lax.fori_loop(0, chunks, lambda c, carry: (body(c), carry)[1], 0)
+
+    @each_chunk
+    def _(c):
+        for side in (0, 1):
+
+            @pl.when(can_send(side))
+            def _():
+                w_copy(side, z, c, True).start()
+
+    lse32[...] = lse_ref[0].astype(jnp.float32)
+    delta32[...] = delta_ref[0].astype(jnp.float32)
+    seg_row = seg_ref[:, pl.ds(pl.multiple_of(tok * window, LANES), window)].astype(jnp.float32)
+    seg_col = jnp.transpose(jnp.broadcast_to(seg_row, (LANES, window)))[:, :1]
+    key_id = lax.broadcasted_iota(jnp.int32, (window, window), 0)
+    query_id = lax.broadcasted_iota(jnp.int32, (window, window), 1)
+    bias[...] = jnp.where((seg_col == seg_row) & (key_id <= query_id), 0.0, -1e30)
+    dk_acc[...] = jnp.zeros_like(dk_acc)
+    dv_acc[...] = jnp.zeros_like(dv_acc)
+    scale = head_size ** (-0.5)
+    half = window // 2
+
+    def dot(a, b, da, db):
+        return lax.dot_general(a, b, (((da,), (db,)), ((), ())), preferred_element_type=jnp.float32)
+
+    @pl.loop(0, groups)
+    def _(r):
+        cols = pl.ds(pl.multiple_of(r * head_size, head_size), head_size)
+        pieces = []
+        for first in (0, half):
+            keys, queries = slice(first, first + half), slice(first, window)
+            q, do = q_ref[queries, cols], do_ref[queries, cols]
+            kk, vv = k_ref[keys, :], v_ref[keys, :]
+            logits = dot(kk, q, 1, 1) * scale - lse32[pl.ds(r, 1), queries]
+            probs = jnp.exp(logits + bias[keys, queries])
+            dv_acc[keys, :] += dot(probs.astype(jnp.bfloat16), do, 1, 0)
+            grad_prob = dot(vv, do, 1, 1)
+            ds = (probs * (grad_prob - delta32[pl.ds(r, 1), queries])).astype(jnp.bfloat16)
+            dk_acc[keys, :] += dot(ds, q, 1, 0)
+            pieces.append(dot(ds, kk, 0, 0))
+        low = pieces[0]
+        joined[y, :half, cols] = (low[:half] * scale).astype(jnp.bfloat16)
+        joined[y, half:, cols] = ((low[half:] + pieces[1]) * scale).astype(jnp.bfloat16)
+
+    wide = groups * head_size
+    joined[y, :, wide : wide + head_size] = (dk_acc[...] * scale).astype(jnp.bfloat16)
+    joined[y, :, wide + head_size : wide + 2 * head_size] = dv_acc[...].astype(jnp.bfloat16)
+
+    def p_copy(o, c, yd):
+        return remote(
+            part.at[o, c, yd], got.at[h, c, yd], p_send.at[o, c, yd], p_recv.at[h, c, yd], tok, o
+        )
+
+    def piece(o, c, yd, own):
+        w = w_ref[own_w(c), :] if own else w_all[o, c]
+        part[o, c, yd] = dot(joined[yd], w, 1, 1).astype(jnp.bfloat16)
+
+    def send_piece(o, c, yd):
+        @pl.when(o != h)
+        def _():
+            p_copy(o, c, yd).start()
+
+    def arrive(side, s, c):
+        o = z + s if side == 0 else z - s
+        w_copy(side, o, c, False).wait_recv()
+
+        @pl.when(can_send(side))
+        def _():
+            w_copy(side, o, c, False).start()
+
+        return o
+
+    def valid(side, s):
+        return z + s < outer if side == 0 else z >= s
+
+    def f_copy(c):
+        return remote(fwd_out.at[c], fwd_in.at[c], f_send.at[c], f_recv.at[c], z * inner + yo, h)
+
+    def total(c, yd):
+        acc = part[h, c, yd].astype(jnp.float32)
+        for step in range(1, heads):
+            g = peer(step)
+            remote(
+                part.at[h, c, yd], got.at[g, c, yd], p_send.at[h, c, yd], p_recv.at[g, c, yd], tok, g
+            ).wait_recv()
+            acc += got[g, c, yd].astype(jnp.float32)
+        return acc.astype(jnp.bfloat16)
+
+    def out_cols(c, yd):
+        return pl.ds(pl.multiple_of(yd * rows + c * LANES, LANES), LANES)
+
+    def reduce_chunk(c):
+        fwd_out[c] = total(c, yo)
+        f_copy(c).start()
+        out_ref[:, out_cols(c, y)] = total(c, y)
+
+    distance = jnp.abs(z - h)
+    j_copy = remote(joined.at[y], joined.at[y], j_send, j_recv, z * inner + yo, h)
+    j_copy.start()
+
+    @each_chunk
+    def _(c):
+        piece(z, c, y, True)
+        send_piece(z, c, y)
+
+    @each_chunk
+    def _(c):
+        for side in (0, 1):
+
+            @pl.when(valid(side, 1))
+            def _():
+                o = arrive(side, 1, c)
+                piece(o, c, y, False)
+                send_piece(o, c, y)
+
+    remote(joined.at[yo], joined.at[yo], j_send, j_recv, z * inner + yo, h).wait_recv()
+
+    @each_chunk
+    def _(c):
+        piece(z, c, yo, True)
+        send_piece(z, c, yo)
+        for side in (0, 1):
+
+            @pl.when(valid(side, 1))
+            def _():
+                o = z + 1 if side == 0 else z - 1
+                piece(o, c, yo, False)
+                send_piece(o, c, yo)
+
+    @pl.when(distance == 0)
+    def _():
+        each_chunk(reduce_chunk)
+
+    for s in range(2, outer):
+
+        @each_chunk
+        def _(c):
+            for side in (0, 1):
+
+                @pl.when(valid(side, s))
+                def _():
+                    o = arrive(side, s, c)
+                    piece(o, c, yo, False)
+                    piece(o, c, y, False)
+                    send_piece(o, c, yo)
+                    send_piece(o, c, y)
+
+            @pl.when(distance == s - 1)
+            def _():
+                reduce_chunk(c)
+
+    @pl.when(distance == outer - 1)
+    def _():
+        each_chunk(reduce_chunk)
+
+    @each_chunk
+    def _(c):
+        f_copy(c).wait_recv()
+        out_ref[:, out_cols(c, yo)] = fwd_in[c]
+
+    j_copy.wait_send()
+
+    @each_chunk
+    def _(c):
+        f_copy(c).wait_send()
+        for step in range(1, heads):
+            for yd in range(inner):
+                p_copy(peer(step), c, yd).wait_send()
+        for side in (0, 1):
+            for s in range(outer):
+
+                @pl.when(can_send(side) & valid(side, s))
+                def _():
+                    w_copy(side, z + s if side == 0 else z - s, c, s == 0).wait_send()
+
+
+def fused(inner, outer, q, k, v, do, lse, delta, segments, weight):
+    window, _, query_width = q.shape
+    head_size = k.shape[2]
+    rows, _, width = weight.shape
+    chunks = rows // LANES
+    bf16, f32 = jnp.bfloat16, jnp.float32
+    dma = pltpu.SemaphoreType.DMA
+    vmem = pl.BlockSpec(memory_space=pltpu.VMEM)
+    return pl.pallas_call(
+        functools.partial(fused_kernel, inner),
+        out_shape=jax.ShapeDtypeStruct((window, inner * rows), bf16),
+        in_specs=[vmem] * 8,
+        out_specs=vmem,
+        scratch_shapes=[
+            pltpu.VMEM((inner, window, width), bf16),
+            pltpu.VMEM((outer, chunks, LANES, width), bf16),
+            pltpu.VMEM((outer, chunks, inner, window, LANES), bf16),
+            pltpu.VMEM((outer, chunks, inner, window, LANES), bf16),
+            pltpu.VMEM((chunks, window, LANES), bf16),
+            pltpu.VMEM((chunks, window, LANES), bf16),
+            pltpu.VMEM((window, window), f32),
+            pltpu.VMEM(lse.shape[1:], f32),
+            pltpu.VMEM(lse.shape[1:], f32),
+            pltpu.VMEM((window, head_size), f32),
+            pltpu.VMEM((window, head_size), f32),
+            dma((2, outer, chunks)),
+            dma((outer, chunks)),
+            dma,
+            dma,
+            dma((outer, chunks, inner)),
+            dma((outer, chunks, inner)),
+            dma((chunks,)),
+            dma((chunks,)),
+        ],
+        compiler_params=pltpu.CompilerParams(
+            collective_id=0, has_side_effects=True, vmem_limit_bytes=60 * 1024 * 1024
+        ),
+    )(
+        q.reshape(window, query_width),
+        k.reshape(window, head_size),
+        v.reshape(window, head_size),
+        do.reshape(window, query_width),
+        lse,
+        delta,
+        segments.reshape(1, -1),
+        weight.reshape(rows, width),
+    )
+
+
 def solution(mesh):
     placed = (
         P("tok", "head", None),
@@ -127,6 +443,16 @@
         P(),
         P("tok", "head", None),
     )
+    tok, heads = mesh.shape["tok"], mesh.shape["head"]
+
+    def step(*args):
+        window, kv_dev, _ = args[0].shape
+        rows = args[7].shape[0]
+        paired = tok == 2 * heads and heads > 1 and kv_dev == 1
+        if paired and rows % LANES == 0 and window % (2 * LANES) == 0 and args[1].shape[2] == LANES:
+            return fused(tok // heads, heads, *args)
+        return on_device(*args)
+
     return jax.shard_map(
-        on_device, mesh=mesh, in_specs=placed, out_specs=P("tok", "head"), check_vma=False
-    )
+        step, mesh=mesh, in_specs=placed, out_specs=P("tok", "head"), check_vma=False
+    )

time: 224 us -> 110 us (0.49)
  waiting for transfers between devices: 178 us -> 0 us
  Pallas kernels: 0 us -> 107 us
  matrix products: 20.2 us -> 0 us
  between operations: 13.5 us -> 0.01 us
  other arithmetic: 4.45 us -> 0 us
  local copies, waits for them, and re-layouts: 5.3 us -> 2.26 us
    all_gather x1 -> x0, waiting for transfers between devices: 133 us -> none  [on_device(): lax.all_gather(query_key_value_weight, 'tok', axis=0, tiled=True)]
    pallas_call x0 -> x1, Pallas kernels: none -> 107 us  [fused(): pl.pallas_call(functools.partial(fused_kernel, inner), out_shape=jax.Shap...]
    reduce_scatter x1 -> x0, waiting for transfers between devices: 44.7 us -> none  [on_device(): lax.psum_scatter(partial_sum.astype(jnp.bfloat16), 'head', scatter_dimens...]
    dot_general x6 -> x0, matrix products: 20.2 us -> none  [the longest x1 11.2 us: on_device(): lax.dot_general(stacked_gradients, flat_piece, (((1,), (1,)), ((), ())),...]
    another operation x2 -> x0, local copies, waits for them, and re-layouts: 3 us -> none
  transfers between devices with their start and end apart: 2 -> 0, of which waited for: 2 -> 0; matrix products, arithmetic and copies ran while one was open for 8% -> 0% of each run, Pallas kernels for 0% -> 0%
where the time goes in v1:
time: 110 us
  Pallas kernels  107 us (97%)
  local copies, waits for them, and re-layouts  2.26 us (2%)
    pallas_call x1, Pallas kernels, fused(): pl.pallas_call(functools.partial(fused_kernel, inner), out_shape=jax.Shap...  107 us
    unnamed x1, local copies, waits for them, and re-layouts  2.26 us

profile of v1, /device:TPU:24, one launch (start us, length us, event | category | flops | bytes accessed | tf_op | source)
XLA Modules:
  0.0 109.7 jit_solution(15529537904155415853)
XLA Ops:
  0.0 107.4 %shard_map.82 = bf16[512,1024]{1,0:T(8,128)(2,1)} custom-call(bf16[512,1024]{1,0:T(8,128)(2,1)} %bitcast.7, bf16[512,128]{1,0:T(8,128)(2,1)} %bitcast.9, bf16[512,128]{1,0:T(8,128)(2,1)} %bitcast.10, bf16[512,1024]{1,0:T(8,128)(2,1)} %bitcast.8, bf16[1,8,512]{2,1,0:T(8,128)(2,1)} %lse_ref.1, bf16[1,8,512]{2,1,0:T(8,128)(2,1)} %delta_ref.1, ...), custom_call_target="tpu_custom_call" | custom-call | tf_op jit(solution)/shard_map/pallas_call | solution.py:394
  107.4 2.3 %copy.10 = bf16[512,1024]{1,0:T(8,128)(2,1)} copy(bf16[512,1024]{1,0:T(8,128)(2,1)} %shard_map.82) | data formatting | bytes 2097152

commit v2 on v1

--- a/solution.py
+++ b/solution.py
@@ -180,7 +180,10 @@
     barrier = pltpu.get_barrier_semaphore()
     pl.semaphore_signal(barrier, inc=1, device_id=(z * inner + yo, h), device_id_type=MESH)
     for step in range(1, heads):
-        pl.semaphore_signal(barrier, inc=1, device_id=(tok, peer(step)), device_id_type=MESH)
+        for to_y in (y, yo):
+            pl.semaphore_signal(
+                barrier, inc=1, device_id=(z * inner + to_y, peer(step)), device_id_type=MESH
+            )
 
     @pl.when(z > 0)
     def _():
@@ -191,7 +194,7 @@
         pl.semaphore_signal(barrier, inc=1, device_id=(tok + inner, h), device_id_type=MESH)
 
     edges = jnp.where(z > 0, 1, 0) + jnp.where(z < outer - 1, 1, 0)
-    pl.semaphore_wait(barrier, heads + edges)
+    pl.semaphore_wait(barrier, 2 * heads - 1 + edges)
 
     def own_w(c):
         return pl.ds(pl.multiple_of(c * LANES, LANES), LANES)
@@ -260,6 +263,16 @@
             part.at[o, c, yd], got.at[h, c, yd], p_send.at[o, c, yd], p_recv.at[h, c, yd], tok, o
         )
 
+    def direct_copy(o, c, yd):
+        return remote(
+            part.at[o, c, yd],
+            got.at[h, c, y],
+            p_send.at[o, c, yd],
+            p_recv.at[h, c, y],
+            z * inner + yd,
+            o,
+        )
+
     def piece(o, c, yd, own):
         w = w_ref[own_w(c), :] if own else w_all[o, c]
         part[o, c, yd] = dot(joined[yd], w, 1, 1).astype(jnp.bfloat16)
@@ -351,27 +364,52 @@
                     o = arrive(side, s, c)
                     piece(o, c, yo, False)
                     piece(o, c, y, False)
-                    send_piece(o, c, yo)
-                    send_piece(o, c, y)
+                    if s < outer - 1:
+                        send_piece(o, c, yo)
+                        send_piece(o, c, y)
+                    else:
+                        direct_copy(o, c, yo).start()
+
+                        @pl.when(o != h)
+                        def _():
+                            direct_copy(o, c, y).start()
 
             @pl.when(distance == s - 1)
             def _():
                 reduce_chunk(c)
 
+    def arrived(g, c, ys):
+        remote(
+            part.at[h, c, ys], got.at[g, c, ys], p_send.at[h, c, ys], p_recv.at[g, c, ys], tok, g
+        ).wait_recv()
+        return got[g, c, ys].astype(jnp.float32)
+
     @pl.when(distance == outer - 1)
     def _():
-        each_chunk(reduce_chunk)
+        @each_chunk
+        def _(c):
+            acc = part[h, c, y].astype(jnp.float32)
+            for step in range(1, heads):
+                acc += arrived(peer(step), c, y)
+            out_ref[:, out_cols(c, y)] = acc.astype(jnp.bfloat16)
+            other = arrived(h, c, yo)
+            for step in range(1, heads):
+                other += arrived(peer(step), c, yo)
+            out_ref[:, out_cols(c, yo)] = other.astype(jnp.bfloat16)
+            direct_copy(h, c, yo).wait_send()
+
+    @pl.when(distance < outer - 1)
+    def _():
+        @each_chunk
+        def _(c):
+            f_copy(c).wait_recv()
+            out_ref[:, out_cols(c, yo)] = fwd_in[c]
+            f_copy(c).wait_send()
+
+    j_copy.wait_send()
 
     @each_chunk
     def _(c):
-        f_copy(c).wait_recv()
-        out_ref[:, out_cols(c, yo)] = fwd_in[c]
-
-    j_copy.wait_send()
-
-    @each_chunk
-    def _(c):
-        f_copy(c).wait_send()
         for step in range(1, heads):
             for yd in range(inner):
                 p_copy(peer(step), c, yd).wait_send()
@@ -448,7 +486,7 @@
     def step(*args):
         window, kv_dev, _ = args[0].shape
         rows = args[7].shape[0]
-        paired = tok == 2 * heads and heads > 1 and kv_dev == 1
+        paired = tok == 2 * heads and heads > 2 and kv_dev == 1
         if paired and rows % LANES == 0 and window % (2 * LANES) == 0 and args[1].shape[2] == LANES:
             return fused(tok // heads, heads, *args)
         return on_device(*args)

time: 110 us -> 108 us (0.982)
  Pallas kernels: 107 us -> 105 us
    pallas_call x1, Pallas kernels: 107 us -> 105 us  [fused(): pl.pallas_call(functools.partial(fused_kernel, inner), out_shape=jax.Shap...]
where the time goes in v2:
time: 108 us
  Pallas kernels  105 us (97%)
  local copies, waits for them, and re-layouts  2.26 us (2%)
    pallas_call x1, Pallas kernels, fused(): pl.pallas_call(functools.partial(fused_kernel, inner), out_shape=jax.Shap...  105 us
    unnamed x1, local copies, waits for them, and re-layouts  2.26 us

profile of v2, /device:TPU:24, one launch (start us, length us, event | category | flops | bytes accessed | tf_op | source)
XLA Modules:
  0.0 107.8 jit_solution(10056471491472461458)
XLA Ops:
  0.0 105.5 %shard_map.82 = bf16[512,1024]{1,0:T(8,128)(2,1)} custom-call(bf16[512,1024]{1,0:T(8,128)(2,1)} %bitcast.7, bf16[512,128]{1,0:T(8,128)(2,1)} %bitcast.9, bf16[512,128]{1,0:T(8,128)(2,1)} %bitcast.10, bf16[512,1024]{1,0:T(8,128)(2,1)} %bitcast.8, bf16[1,8,512]{2,1,0:T(8,128)(2,1)} %lse_ref.1, bf16[1,8,512]{2,1,0:T(8,128)(2,1)} %delta_ref.1, ...), custom_call_target="tpu_custom_call" | custom-call | tf_op jit(solution)/shard_map/pallas_call | solution.py:432
  105.5 2.3 %copy.10 = bf16[512,1024]{1,0:T(8,128)(2,1)} copy(bf16[512,1024]{1,0:T(8,128)(2,1)} %shard_map.82) | data formatting | bytes 2097152

commit v3 on v2

--- a/solution.py
+++ b/solution.py
@@ -456,7 +456,7 @@
             dma((chunks,)),
         ],
         compiler_params=pltpu.CompilerParams(
-            collective_id=0, has_side_effects=True, vmem_limit_bytes=60 * 1024 * 1024
+            collective_id=0, has_side_effects=True, vmem_limit_bytes=36 * 1024 * 1024
         ),
     )(
         q.reshape(window, query_width),

time: 108 us -> 111 us (1.028)
  local copies, waits for them, and re-layouts: 2.26 us -> 8.65 us
  Pallas kernels: 105 us -> 102 us
    unnamed x1 -> x17, local copies, waits for them, and re-layouts: 2.26 us -> 8.65 us
    pallas_call x1, Pallas kernels: 105 us -> 102 us  [fused(): pl.pallas_call(functools.partial(fused_kernel, inner), out_shape=jax.Shap...]
where the time goes in v3:
time: 111 us
  Pallas kernels  102 us (92%)
  local copies, waits for them, and re-layouts  8.65 us (8%)
    pallas_call x1, Pallas kernels, fused(): pl.pallas_call(functools.partial(fused_kernel, inner), out_shape=jax.Shap...  102 us
    unnamed x17, local copies, waits for them, and re-layouts  8.65 us

profile of v3, /device:TPU:24, one launch (start us, length us, event | category | flops | bytes accessed | tf_op | source)
XLA Modules:
  0.0 111.1 jit_solution(9846438205322445528)
XLA Ops:
  0.0 0.0 copy-start
  0.0 1.3 %copy-done = bf16[512,1,1280]{2,0,1:T(8,128)(2,1)S(1)} copy-done((bf16[512,1,1280]{2,0,1:T(8,128)(2,1)S(1)}, bf16[512,1,1280]{2,0,1:T(8,128)(2,1)}, u32[]{:S(2)}) %copy-start) | copy-done | bytes 1310744
  1.3 0.0 copy-start.1
  1.3 1.2 %copy-done.1 = bf16[512,1,1024]{2,0,1:T(8,128)(2,1)S(1)} copy-done((bf16[512,1,1024]{2,0,1:T(8,128)(2,1)S(1)}, bf16[512,1,1024]{2,0,1:T(8,128)(2,1)}, u32[]{:S(2)}) %copy-start.1) | copy-done | bytes 1048600
  2.5 0.0 copy-start.2
  2.5 1.2 %copy-done.2 = bf16[512,1,1024]{2,0,1:T(8,128)(2,1)S(1)} copy-done((bf16[512,1,1024]{2,0,1:T(8,128)(2,1)S(1)}, bf16[512,1,1024]{2,0,1:T(8,128)(2,1)}, u32[]{:S(2)}) %copy-start.2) | copy-done | bytes 1048600
  3.8 0.0 copy-start.3
  3.8 0.9 copy-done.3
  4.7 0.0 copy-start.4
  4.7 0.9 copy-done.4
  5.6 0.0 copy-start.5
  5.6 0.7 copy-done.5
  6.3 0.0 copy-start.6
  6.3 0.7 copy-done.6
  7.0 0.0 copy-start.7
  7.0 0.7 copy-done.7
  7.7 102.4 %shard_map.82 = bf16[512,1024]{1,0:T(8,128)(2,1)S(1)} custom-call(bf16[512,1024]{1,0:T(8,128)(2,1)S(1)} %bitcast.7, bf16[512,128]{1,0:T(8,128)(2,1)S(1)} %bitcast.9, bf16[512,128]{1,0:T(8,128)(2,1)S(1)} %bitcast.10, bf16[512,1024]{1,0:T(8,128)(2,1)S(1)} %bitcast.8, bf16[1,8,512]{2,1,0:T(8,128)(2,1)S(1)} %copy-done.6, bf16[1,8,512]{2,1,0:T(8,128)(2,1)S(1)} %copy-done.7, ...), custom_call_target="tpu_custom_call" | custom-call | tf_op jit(solution)/shard_map/pallas_call | solution.py:432
  110.1 1.0 copy.10
Async XLA Ops:
  0.0 1.3 %copy-start = (bf16[512,1,1280]{2,0,1:T(8,128)(2,1)S(1)}, bf16[512,1,1280]{2,0,1:T(8,128)(2,1)}, u32[]{:S(2)}) copy-start(bf16[512,1,1280]{2,0,1:T(8,128)(2,1)} %param.15) | copy-start | bytes 3932164
  1.3 1.2 %copy-start.1 = (bf16[512,1,1024]{2,0,1:T(8,128)(2,1)S(1)}, bf16[512,1,1024]{2,0,1:T(8,128)(2,1)}, u32[]{:S(2)}) copy-start(bf16[512,1,1024]{2,0,1:T(8,128)(2,1)} %param.8) | copy-start | bytes 3145732
  2.5 1.2 %copy-start.2 = (bf16[512,1,1024]{2,0,1:T(8,128)(2,1)S(1)}, bf16[512,1,1024]{2,0,1:T(8,128)(2,1)}, u32[]{:S(2)}) copy-start(bf16[512,1,1024]{2,0,1:T(8,128)(2,1)} %param.11) | copy-start | bytes 3145732
  3.8 0.9 copy-start.3
  4.7 0.9 copy-start.4
  5.6 0.7 copy-start.5
  6.3 0.7 copy-start.6
  7.0 0.7 copy-start.7
